TPU v7x, 1024 devices: a whole 4x4x32 slice. The times are simulated.
1024 devices in a mesh: head: 8 (over x, z_hi), outer: 4 (over y), inner: 32 (over z_lo, core).
Axes of the slice: x: 4, y: 4, z: 32 (z_hi: 2, z_lo: 16; z = z_hi * 16 + z_lo), core: 2. Of those that a mesh axis runs over, the one named last changes fastest.
Arguments:
- queries: bfloat16 [128, 256, 4096], P(('outer', 'inner'), 'head'), may hold values from -120 to 120
- keys: bfloat16 [128, 256, 1024], P(('outer', 'inner'), 'head'), may hold values from -6 to 6
- values: bfloat16 [128, 256, 1024], P(('outer', 'inner'), 'head'), may hold values from -6 to 6
- doc_lengths: int32 [16], replicated, may hold values from 1 to 4096, 32768 in all
Outputs:
- attended: bfloat16 [128, 256, 4096], P(('outer', 'inner'), 'head')
Inputs may be any that keep to these rules, and one draw needn't show every extreme that they name: `doc_lengths`: the documents of the packed sequence in order, summing to 32768.
All inputs are finite; a program needn't handle non-finite values.
Results may differ from a plain program's by a relative error of at most 0.0044.
Values may be sent and summed in bfloat16 or wider, within the bound.
No kernel may reach another device: no remote copies, remote signals or barrier semaphores. Data moves between devices by JAX's collectives and lax.ppermute only.
A program may use at most 32 MiB of HBM per device.

v0:
```python
import functools
import math

import jax
import jax.numpy as jnp
from jax import lax
from jax.experimental import pallas as pl
from jax.experimental.pallas import tpu as pltpu
from jax.sharding import Mesh
from jax.sharding import PartitionSpec as P


HD = 128
ROWS = 32
HEADS = 4
CHUNK = 64
NEG_FILL = -1e30
AXES = ("x", "zh", "y", "zl", "c")
PLANE = ("x", "c")
RING = ("zh", "y", "zl")

STEPS = (
    ("m1", (0,), (-9,), -9),
    ("p1", (0,), (3,), 3),
    ("p2", (3,), (6,), 3),
    ("m2", (-9,), (-12,), -3),
    ("e1", (0, 3, 6), (1, 4, 7), 1),
    ("m3", (-12,), (-15,), -3),
    ("g1", (-9, -12, 3, 6), (-10, -13, 2, 5), -1),
    ("g2", (-9, -12, 7), (-8, -11, 8), 1),
    ("h1", (-15,), (-16,), -1),
    ("h2", (-15,), (-14,), 1),
)
CALLS = (
    (0, 3, 6),
    (1, 4, 7, -9, -12),
    (2, 5, 8, -10, -13, -8, -11, -15),
    (-16, -14),
)


class Plan:
    def __init__(self, outer, half, halves):
        length, chips = half * halves, outer * half
        index = lambda z, y: ((z // half) * outer + y) * half + z % half
        where = {(z, y * half + z % half): index(z, y) for z in range(length) for y in range(outer)}
        held = {0: {key: key for key in where}}
        self.pairs = {}
        for name, sent, got, shift in STEPS:
            target = {}
            for slot, new in zip(sent, got):
                held[new] = {}
                for (z, n), (zs, ns) in held[slot].items():
                    z2 = (z + shift) % length
                    to = (z2, (ns + (z2 - zs) % half) % chips)
                    assert target.setdefault((z, n), to) == to
                    held[new][to] = (zs, ns)
            assert len(set(target.values())) == len(target)
            self.pairs[name] = [(where[a], where[b]) for a, b in sorted(target.items())]
        for (z, n) in where:
            want = {(h * half + m % half, m) for m in range(max(0, n - half // 2), n + 1) for h in range(halves)}
            got = [held[s][z, n] for call in CALLS for s in call]
            assert len(set(got)) == len(got) and want <= set(got)


def row_offsets(shape, dim):
    i = lax.broadcasted_iota(jnp.int32, shape, dim)
    return ((i >> 5) & 1) * 256 + (i >> 6) * 64 + (i & 31)


def attend_kernel(slots, first, last, *refs):
    count = len(slots)
    refs = list(refs)
    lengths, q_ref = refs[:2]
    refs = refs[2:]
    arrays = max(a for _, a, _ in slots) + 1
    kv, refs = refs[:arrays], refs[arrays:]
    if not first:
        (start_ref, top_in, acc_in), refs = refs[:3], refs[3:]
    if last:
        out_ref, *scores, k_all, v_all, bias, tops = refs
    elif first:
        start_ref, tops, acc_out, *scores, k_all, v_all, bias = refs
    else:
        tops, acc_out, *scores, k_all, v_all, bias = refs
    scores, rounded = scores[:2], scores[2:]
    unit = math.log2(math.e) / math.sqrt(HD)
    half, halves = lax.axis_size("zl"), lax.axis_size("zh")

    chip = lax.axis_index("y") * half + lax.axis_index("zl")
    zh = lax.axis_index("zh")
    low = chip * 512 + zh * ROWS
    reach = 256 + 6 * ROWS + ROWS - 1

    def start_of(pos):
        end, begin = jnp.int32(0), pos * 0
        for d in range(lengths.shape[0]):
            end = end + lengths[d]
            begin = jnp.where(end <= pos, end, begin)
        return begin

    high_start = start_of(low + reach)
    q_pos = low + row_offsets((256, 1), 0)
    if first:
        start_ref[...] = start_of(q_pos)
    partial = []
    for j, (slot, a, i) in enumerate(slots):
        back = slot if slot >= 0 else slot + half
        from_zh = ((zh * half + lax.axis_index("zl") - slot + half * halves) >> 4) & 1
        k_base = (chip - back) * 512 + from_zh * ROWS
        partial.append((k_base < high_start) | (k_base + reach > low))

        @pl.when(partial[j])
        def _(j=j, k_base=k_base):
            k_pos = k_base + row_offsets((1, 256), 1)
            seen = (k_pos <= q_pos) & (k_pos >= start_ref[...])
            bias[:, j * 256 : (j + 1) * 256] = jnp.where(seen, 0.0, NEG_FILL)

        k_all[j * 256 : (j + 1) * 256] = kv[a][i, :, 0].reshape(256, HD)
        v_all[j * 256 : (j + 1) * 256, :HD] = kv[a][i, :, 1].reshape(256, HD)

    v_all[:, HD:] = jnp.ones((count * 256, HD), jnp.bfloat16)

    def score(h):
        q = q_ref[:, h].reshape(256, HD)
        scores[h & 1][...] = lax.dot_general(
            q, k_all[...], (((1,), (1,)), ((), ())), preferred_element_type=jnp.float32
        )

    def hide(h):
        for j in range(count):

            @pl.when(partial[j])
            def _(j=j):
                cols = slice(j * 256, (j + 1) * 256)
                scores[h & 1][:, cols] = scores[h & 1][:, cols] + bias[:, cols]

    def weigh(h):
        for r in range(0, 256, CHUNK):
            rows = slice(r, r + CHUNK)
            wide = scores[h & 1][rows, :256]
            for j in range(1, count):
                wide = jnp.maximum(wide, scores[h & 1][rows, j * 256 : (j + 1) * 256])
            top = jnp.max(wide, axis=1, keepdims=True)
            if not first:
                top = jnp.maximum(top_in[h, rows], top)
            for j in range(count):
                cols = slice(j * 256, (j + 1) * 256)
                w = jnp.exp2((scores[h & 1][rows, cols] - top) * unit)
                rounded[h & 1][rows, cols] = w.astype(jnp.bfloat16)
            tops[h, rows] = top

    def gather(h):
        for r in range(0, 256, 128):
            rows = slice(r, r + 128)
            added = jnp.dot(rounded[h & 1][rows], v_all[...], preferred_element_type=jnp.float32)
            if not first:
                factor = jnp.exp2((top_in[h, rows] - tops[h, rows]) * unit)
                added = added + acc_in[h, rows] * factor
            if last:
                res = added[:, :HD] / added[:, HD:]
                out_ref[r // ROWS : r // ROWS + 4, h] = res.astype(jnp.bfloat16).reshape(4, ROWS, HD)
            else:
                acc_out[h, rows] = added

    for h in range(HEADS + 2):
        if h < HEADS:
            score(h)
        if h >= 2:
            gather(h - 2)
        if 1 <= h <= HEADS:
            weigh(h - 1)
        if h < HEADS:
            hide(h)


VMEM = pl.BlockSpec(memory_space=pltpu.VMEM)
SMEM = pl.BlockSpec(memory_space=pltpu.SMEM)


def attend(lengths, q, slots, blocks, state, last):
    n = len(blocks)
    first = state is None
    start = jax.ShapeDtypeStruct((256, 1), jnp.int32)
    top = jax.ShapeDtypeStruct((HEADS, 256, 1), jnp.float32)
    acc = jax.ShapeDtypeStruct((HEADS, 256, 2 * HD), jnp.float32)
    out = jax.ShapeDtypeStruct((8, HEADS, ROWS, HD), jnp.bfloat16)
    outs = out if last else (start, top, acc) if first else (top, acc)
    arrays = list({id(b): b for b, _ in blocks}.values())
    number = {id(b): a for a, b in enumerate(arrays)}
    where = tuple((s, number[id(b)], i) for s, (b, i) in zip(slots, blocks))
    return pl.pallas_call(
        functools.partial(attend_kernel, where, first, last),
        out_shape=outs,
        in_specs=[SMEM, VMEM] + [VMEM] * len(arrays) + ([] if first else [VMEM] * 3),
        out_specs=VMEM if last else tuple(VMEM for _ in outs),
        scratch_shapes=[
            pltpu.VMEM((256, n * 256), jnp.float32),
            pltpu.VMEM((256, n * 256), jnp.float32),
            pltpu.VMEM((256, n * 256), jnp.bfloat16),
            pltpu.VMEM((256, n * 256), jnp.bfloat16),
            pltpu.VMEM((n * 256, HD), jnp.bfloat16),
            pltpu.VMEM((n * 256, 2 * HD), jnp.bfloat16),
            pltpu.VMEM((256, n * 256), jnp.float32),
        ]
        + ([pltpu.VMEM(top.shape, top.dtype)] if last else []),
        compiler_params=pltpu.CompilerParams(vmem_limit_bytes=(6 + 2 * n) << 20),
        cost_estimate=pl.CostEstimate(
            flops=n * HEADS * 256 * 256 * HD * 4,
            bytes_accessed=n * 131072 + 1500000,
            transcendentals=n * HEADS * 256 * 256,
        ),
    )(lengths, q, *arrays, *(() if first else state))


def pack_kv_kernel(k_ref, v_ref, out_ref):
    for g in range(8):
        out_ref[g, 0] = k_ref[0, :, g * HD : (g + 1) * HD]
        out_ref[g, 1] = v_ref[0, :, g * HD : (g + 1) * HD]


def pack_q_kernel(q_ref, out_ref):
    for g in range(8):
        for h in range(HEADS):
            at = (g * HEADS + h) * HD
            out_ref[g, h] = q_ref[0, :, at : at + HD]


def pack(kernel, shape, *arrays):
    return pl.pallas_call(
        kernel,
        out_shape=jax.ShapeDtypeStruct(shape, jnp.bfloat16),
        in_specs=[VMEM] * len(arrays),
        out_specs=VMEM,
    )(*arrays)


def body(plan, *args):
    return spread(plan, *args)


def spread(plan, queries, keys, values, doc_lengths):
    kv = pack(pack_kv_kernel, (8, 2, ROWS, HD), keys, values)
    own = lax.all_to_all(kv, PLANE, split_axis=0, concat_axis=0, tiled=True)
    q = pack(pack_q_kernel, (8, HEADS, ROWS, HD), queries)
    q = lax.all_to_all(q, PLANE, split_axis=0, concat_axis=0, tiled=True)

    held = {0: (own[None], 0)}
    for name, sent, got, _ in STEPS:
        parts = [held[s][0][held[s][1]] for s in sent]
        back = lax.ppermute(jnp.stack(parts), RING, plan.pairs[name])
        for i, s in enumerate(got):
            held[s] = (back, i)

    state, start = None, None
    for j, call in enumerate(CALLS):
        state = attend(doc_lengths, q, call, [held[s] for s in call], state, j == len(CALLS) - 1)
        if j == 0:
            start, *state = state
        if j < len(CALLS) - 1:
            state = (start, *state)
    out = lax.all_to_all(state, PLANE, split_axis=0, concat_axis=0, tiled=True)
    return jnp.transpose(out, (2, 0, 1, 3)).reshape(1, ROWS, 32 * HD)


def solution(mesh):
    fine = Mesh(mesh.devices.reshape(4, 2, 4, 16, 2), AXES)
    spec = P(("y", "zl", "c"), ("x", "zh"), None)
    return jax.shard_map(
        functools.partial(body, Plan(4, 16, 2)),
        mesh=fine,
        in_specs=(spec, spec, spec, P()),
        out_specs=spec,
        check_vma=False,
    )
```

profile of v0, /device:TPU:1, one launch (start us, length us, event | category | flops | bytes accessed | tf_op | source)
XLA Modules:
  0.0 157.6 jit_solution(8455968548664788064)
XLA Ops:
  0.0 1.5 shard_map.47
  1.6 22.6 %all_to_all.15 = bf16[8,2,32,128]{3,2,1,0:T(8,128)(2,1)S(1)} all-to-all(bf16[8,2,32,128]{3,2,1,0:T(8,128)(2,1)} %shard_map.47), channel_id=1, replica_groups=mesh['x'=4,'zh'=2,'y'=4,'zl'=16,'c'=2] {'x','c'}, dimensions={0} | all-to-all | bytes 262144 | tf_op jit(solution)/shard_map/all_to_all | solution.py:244
  24.2 1.9 %collective-permute-start.5 = (bf16[1,8,2,32,128]{4,3,2,1,0:T(8,128)(2,1)S(1)}, bf16[1,8,2,32,128]{4,3,2,1,0:T(8,128)(2,1)S(1)}, u32[]{:S(2)}, u32[]{:S(2)}) collective-permute-start(bf16[1,8,2,32,128]{4,3,2,1,0:T(8,128)(2,1)S(1)} %bitcast.2), channel_id=1, source_target_pairs={{0,6},{32,38},{64,70},{96,102},{2,8},{34,40},{66,72},{98,104},{4,1... | collective-permute-start | bytes 393224 | tf_op jit(solution)/shard_map/ppermute | solution.py:251
  26.1 11.3 %collective-permute-done.5.refs_3_ = bf16[1,8,2,32,128]{4,3,2,1,0:T(8,128)(2,1)S(1)} collective-permute-done((bf16[1,8,2,32,128]{4,3,2,1,0:T(8,128)(2,1)S(1)}, bf16[1,8,2,32,128]{4,3,2,1,0:T(8,128)(2,1)S(1)}, u32[]{:S(2)}, u32[]{:S(2)}) %collective-permute-start.5) | collective-permute-done | bytes 131104 | tf_op jit(solution)/shard_map/ppermute | solution.py:251
  37.4 1.9 %collective-permute-start.6 = (bf16[1,8,2,32,128]{4,3,2,1,0:T(8,128)(2,1)S(1)}, bf16[1,8,2,32,128]{4,3,2,1,0:T(8,128)(2,1)S(1)}, u32[]{:S(2)}, u32[]{:S(2)}) collective-permute-start(bf16[1,8,2,32,128]{4,3,2,1,0:T(8,128)(2,1)S(1)} %collective-permute-done.5.refs_3_), channel_id=1, source_target_pairs={{0,6},{32,38},{64,70},{96,102},{2,8},{34,40},{66,72},{98,104},{4,1... | collective-permute-start | bytes 393224 | tf_op jit(solution)/shard_map/ppermute | solution.py:251
  39.4 13.3 %collective-permute-start = (bf16[1,8,2,32,128]{4,3,2,1,0:T(8,128)(2,1)S(1)}, bf16[1,8,2,32,128]{4,3,2,1,0:T(8,128)(2,1)S(1)}, u32[]{:S(2)}, u32[]{:S(2)}) collective-permute-start(bf16[1,8,2,32,128]{4,3,2,1,0:T(8,128)(2,1)S(1)} %bitcast.3), channel_id=1, source_target_pairs={{0,142},{32,174},{64,206},{96,238},{2,144},{34,176},{66,208},{98,2... | collective-permute-start | bytes 393224 | tf_op jit(solution)/shard_map/ppermute | solution.py:251
  52.6 0.0 collective-permute-done.6.refs_4_
  52.7 3.5 %collective-permute-start.8 = (bf16[3,8,2,32,128]{4,3,2,1,0:T(8,128)(2,1)S(1)}, bf16[3,8,2,32,128]{4,3,2,1,0:T(8,128)(2,1)S(1)}, u32[]{:S(2)}, u32[]{:S(2)}) collective-permute-start(bf16[3,8,2,32,128]{4,3,2,1,0:T(8,128)(2,1)S(1)} %pad_maximum_fusion.1), channel_id=1, source_target_pairs={{0,2},{32,34},{64,66},{96,98},{2,4},{34,36},{66,68},{98,100},{4,6}... | collective-permute-start | bytes 1179656 | tf_op jit(solution)/shard_map/ppermute | solution.py:251
  56.3 6.0 %collective-permute-done.refs_3_ = bf16[1,8,2,32,128]{4,3,2,1,0:T(8,128)(2,1)S(1)} collective-permute-done((bf16[1,8,2,32,128]{4,3,2,1,0:T(8,128)(2,1)S(1)}, bf16[1,8,2,32,128]{4,3,2,1,0:T(8,128)(2,1)S(1)}, u32[]{:S(2)}, u32[]{:S(2)}) %collective-permute-start) | collective-permute-done | bytes 131104 | tf_op jit(solution)/shard_map/ppermute | solution.py:251
  62.2 22.3 %collective-permute-start.1 = (bf16[1,8,2,32,128]{4,3,2,1,0:T(8,128)(2,1)S(1)}, bf16[1,8,2,32,128]{4,3,2,1,0:T(8,128)(2,1)S(1)}, u32[]{:S(2)}, u32[]{:S(2)}) collective-permute-start(bf16[1,8,2,32,128]{4,3,2,1,0:T(8,128)(2,1)S(1)} %collective-permute-done.refs_3_), channel_id=1, source_target_pairs={{0,250},{32,154},{64,186},{96,218},{2,252},{34,156},{66,188},{98,2... | collective-permute-start | bytes 393224 | tf_op jit(solution)/shard_map/ppermute | solution.py:251
  84.5 6.0 %collective-permute-done.1.refs_4_ = bf16[1,8,2,32,128]{4,3,2,1,0:T(8,128)(2,1)S(1)} collective-permute-done((bf16[1,8,2,32,128]{4,3,2,1,0:T(8,128)(2,1)S(1)}, bf16[1,8,2,32,128]{4,3,2,1,0:T(8,128)(2,1)S(1)}, u32[]{:S(2)}, u32[]{:S(2)}) %collective-permute-start.1) | collective-permute-done | bytes 131104 | tf_op jit(solution)/shard_map/ppermute | solution.py:251
  90.5 0.1 pad_maximum_fusion
  90.6 1.9 %collective-permute-start.7 = (bf16[4,8,2,32,128]{4,3,2,1,0:T(8,128)(2,1)S(1)}, bf16[4,8,2,32,128]{4,3,2,1,0:T(8,128)(2,1)S(1)}, u32[]{:S(2)}, u32[]{:S(2)}) collective-permute-start(bf16[4,8,2,32,128]{4,3,2,1,0:T(8,128)(2,1)S(1)} %pad_maximum_fusion), channel_id=1, source_target_pairs={{0,254},{32,158},{64,190},{96,222},{2,0},{34,32},{66,64},{98,96},{... | collective-permute-start | bytes 1572872 | tf_op jit(solution)/shard_map/ppermute | solution.py:251
  92.5 0.0 collective-permute-done.8.refs_2_
  92.6 3.4 %collective-permute-start.9 = (bf16[3,8,2,32,128]{4,3,2,1,0:T(8,128)(2,1)S(1)}, bf16[3,8,2,32,128]{4,3,2,1,0:T(8,128)(2,1)S(1)}, u32[]{:S(2)}, u32[]{:S(2)}) collective-permute-start(bf16[3,8,2,32,128]{4,3,2,1,0:T(8,128)(2,1)S(1)} %pad_maximum_fusion.2), channel_id=1, source_target_pairs={{0,2},{32,34},{64,66},{96,98},{2,4},{34,36},{66,68},{98,100},{4,6}... | collective-permute-start | bytes 1179656 | tf_op jit(solution)/shard_map/ppermute | solution.py:251
  96.0 1.7 %shard_map.46 = bf16[8,4,32,128]{3,2,1,0:T(8,128)(2,1)} custom-call(bf16[1,32,4096]{2,1,0:T(8,128)(2,1)} %q_ref.1), custom_call_target="tpu_custom_call" | custom-call | tf_op jit(solution)/shard_map/pallas_call | solution.py:230
  97.7 0.0 copy-start
  97.7 7.6 %all-to-all-start = ((bf16[8,4,32,128]{3,2,1,0:T(8,128)(2,1)}), bf16[8,4,32,128]{3,2,1,0:T(8,128)(2,1)S(1)}, u32[]{:S(2)}, u32[]{:S(2)}) async-start(bf16[8,4,32,128]{3,2,1,0:T(8,128)(2,1)} %shard_map.46), calls=%async_computation | async-start | bytes 524288 | tf_op jit(solution)/shard_map/all_to_all | solution.py:246
  105.3 7.1 %collective-permute-start.2 = (bf16[1,8,2,32,128]{4,3,2,1,0:T(8,128)(2,1)S(1)}, bf16[1,8,2,32,128]{4,3,2,1,0:T(8,128)(2,1)S(1)}, u32[]{:S(2)}, u32[]{:S(2)}) collective-permute-start(bf16[1,8,2,32,128]{4,3,2,1,0:T(8,128)(2,1)S(1)} %collective-permute-done.1.refs_4_), channel_id=1, source_target_pairs={{0,250},{32,154},{64,186},{96,218},{2,252},{34,156},{66,188},{98,2... | collective-permute-start | bytes 393224 | tf_op jit(solution)/shard_map/ppermute | solution.py:251
  112.5 0.0 all-to-all-done.refs_1_
  112.5 0.0 copy-done
  112.5 3.2 %shard_map.48 = (s32[256,1]{1,0:T(8,128)S(1)}, f32[4,256,1]{2,1,0:T(8,128)S(1)}, f32[4,256,256]{2,1,0:T(8,128)S(1)}) custom-call(s32[16]{0:T(128)S(1)} %copy-done, bf16[8,4,32,128]{3,2,1,0:T(8,128)(2,1)S(1)} %all-to-all-done.refs_1_, bf16[1,8,2,32,128]{4,3,2,1,0:T(8,128)(2,1)S(1)} %bitcast.5, bf16[1,8,2,32,128]{4,3,2,1,0:T(8,128)(2,1)S(1)} %collective-permute-done.5.refs_3_, ...), custom_call_target="tpu_custom_call" | custom-call | flops 402653184 | bytes 1893216 | tf_op jit(solution)/shard_map/pallas_call | solution.py:192
  115.7 5.8 %collective-permute-done.2.refs_4_ = bf16[1,8,2,32,128]{4,3,2,1,0:T(8,128)(2,1)S(1)} collective-permute-done((bf16[1,8,2,32,128]{4,3,2,1,0:T(8,128)(2,1)S(1)}, bf16[1,8,2,32,128]{4,3,2,1,0:T(8,128)(2,1)S(1)}, u32[]{:S(2)}, u32[]{:S(2)}) %collective-permute-start.2) | collective-permute-done | bytes 131104 | tf_op jit(solution)/shard_map/ppermute | solution.py:251
  121.5 7.4 %collective-permute-start.3 = (bf16[1,8,2,32,128]{4,3,2,1,0:T(8,128)(2,1)S(1)}, bf16[1,8,2,32,128]{4,3,2,1,0:T(8,128)(2,1)S(1)}, u32[]{:S(2)}, u32[]{:S(2)}) collective-permute-start(bf16[1,8,2,32,128]{4,3,2,1,0:T(8,128)(2,1)S(1)} %collective-permute-done.2.refs_4_), channel_id=1, source_target_pairs={{0,254},{32,158},{64,190},{96,222},{2,0},{34,32},{66,64},{98,96},{... | collective-permute-start | bytes 393224 | tf_op jit(solution)/shard_map/ppermute | solution.py:251
  128.9 1.9 %collective-permute-start.4 = (bf16[1,8,2,32,128]{4,3,2,1,0:T(8,128)(2,1)S(1)}, bf16[1,8,2,32,128]{4,3,2,1,0:T(8,128)(2,1)S(1)}, u32[]{:S(2)}, u32[]{:S(2)}) collective-permute-start(bf16[1,8,2,32,128]{4,3,2,1,0:T(8,128)(2,1)S(1)} %collective-permute-done.2.refs_4_), channel_id=1, source_target_pairs={{0,2},{32,34},{64,66},{96,98},{2,4},{34,36},{66,68},{98,100},{4,6}... | collective-permute-start | bytes 393224 | tf_op jit(solution)/shard_map/ppermute | solution.py:251
  130.8 4.3 %shard_map.49 = (f32[4,256,1]{2,1,0:T(8,128)S(1)}, f32[4,256,256]{2,1,0:T(8,128)S(1)}) custom-call(s32[16]{0:T(128)S(1)} %copy-done, bf16[8,4,32,128]{3,2,1,0:T(8,128)(2,1)S(1)} %all-to-all-done.refs_1_, bf16[3,8,2,32,128]{4,3,2,1,0:T(8,128)(2,1)S(1)} %collective-permute-done.8.refs_2_, bf16[1,8,2,32,128]{4,3,2,1,0:T(8,128)(2,1)S(1)} %collective-permute-done.refs_3_, ...), custom_call_target="tpu_custom_call" | custom-call | flops 671088640 | bytes 2155360 | tf_op jit(solution)/shard_map/pallas_call | solution.py:192
  135.2 0.0 collective-permute-done.7.refs_2_
  135.2 0.0 collective-permute-done.9.refs_3_
  135.2 6.8 %shard_map.50 = (f32[4,256,1]{2,1,0:T(8,128)S(1)}, f32[4,256,256]{2,1,0:T(8,128)S(1)}) custom-call(s32[16]{0:T(128)S(1)} %copy-done, bf16[8,4,32,128]{3,2,1,0:T(8,128)(2,1)S(1)} %all-to-all-done.refs_1_, bf16[4,8,2,32,128]{4,3,2,1,0:T(8,128)(2,1)S(1)} %collective-permute-done.7.refs_2_, bf16[3,8,2,32,128]{4,3,2,1,0:T(8,128)(2,1)S(1)} %collective-permute-done.9.refs_3_, ...), custom_call_target="tpu_custom_call" | custom-call | flops 1073741824 | bytes 2548576 | tf_op jit(solution)/shard_map/pallas_call | solution.py:192
  142.1 0.0 collective-permute-done.3.refs_2_
  142.1 0.0 collective-permute-done.4.refs_3_
  142.1 2.7 %shard_map.51 = bf16[8,4,32,128]{3,2,1,0:T(8,128)(2,1)S(1)} custom-call(s32[16]{0:T(128)S(1)} %copy-done, bf16[8,4,32,128]{3,2,1,0:T(8,128)(2,1)S(1)} %all-to-all-done.refs_1_, bf16[1,8,2,32,128]{4,3,2,1,0:T(8,128)(2,1)S(1)} %collective-permute-done.3.refs_2_, bf16[1,8,2,32,128]{4,3,2,1,0:T(8,128)(2,1)S(1)} %collective-permute-done.4.refs_3_, ...), custom_call_target="tpu_custom_call" | custom-call | flops 268435456 | bytes 1762144 | tf_op jit(solution)/shard_map/pallas_call | solution.py:192
  144.8 11.8 %all_to_all.16 = bf16[8,4,32,128]{3,2,1,0:T(8,128)(2,1)S(1)} all-to-all(bf16[8,4,32,128]{3,2,1,0:T(8,128)(2,1)S(1)} %shard_map.51), channel_id=1, replica_groups=mesh['x'=4,'zh'=2,'y'=4,'zl'=16,'c'=2] {'x','c'}, dimensions={0} | all-to-all | bytes 524288 | tf_op jit(solution)/shard_map/all_to_all | solution.py:262
  156.6 0.1 copy.5
  156.7 0.9 reshape.3
  (3 shorter events, 0.1 us)
Async XLA Ops:
  24.2 13.3 %collective-permute-start.5 = (bf16[1,8,2,32,128]{4,3,2,1,0:T(8,128)(2,1)S(1)}, bf16[1,8,2,32,128]{4,3,2,1,0:T(8,128)(2,1)S(1)}, u32[]{:S(2)}, u32[]{:S(2)}) collective-permute-start(bf16[1,8,2,32,128]{4,3,2,1,0:T(8,128)(2,1)S(1)} %bitcast.2), channel_id=1, source_target_pairs={{0,6},{32,38},{64,70},{96,102},{2,8},{34,40},{66,72},{98,104},{4,1... | collective-permute-start | bytes 393224 | tf_op jit(solution)/shard_map/ppermute | solution.py:251
  37.4 15.2 %collective-permute-start.6 = (bf16[1,8,2,32,128]{4,3,2,1,0:T(8,128)(2,1)S(1)}, bf16[1,8,2,32,128]{4,3,2,1,0:T(8,128)(2,1)S(1)}, u32[]{:S(2)}, u32[]{:S(2)}) collective-permute-start(bf16[1,8,2,32,128]{4,3,2,1,0:T(8,128)(2,1)S(1)} %collective-permute-done.5.refs_3_), channel_id=1, source_target_pairs={{0,6},{32,38},{64,70},{96,102},{2,8},{34,40},{66,72},{98,104},{4,1... | collective-permute-start | bytes 393224 | tf_op jit(solution)/shard_map/ppermute | solution.py:251
  39.4 22.9 %collective-permute-start = (bf16[1,8,2,32,128]{4,3,2,1,0:T(8,128)(2,1)S(1)}, bf16[1,8,2,32,128]{4,3,2,1,0:T(8,128)(2,1)S(1)}, u32[]{:S(2)}, u32[]{:S(2)}) collective-permute-start(bf16[1,8,2,32,128]{4,3,2,1,0:T(8,128)(2,1)S(1)} %bitcast.3), channel_id=1, source_target_pairs={{0,142},{32,174},{64,206},{96,238},{2,144},{34,176},{66,208},{98,2... | collective-permute-start | bytes 393224 | tf_op jit(solution)/shard_map/ppermute | solution.py:251
  52.7 39.8 %collective-permute-start.8 = (bf16[3,8,2,32,128]{4,3,2,1,0:T(8,128)(2,1)S(1)}, bf16[3,8,2,32,128]{4,3,2,1,0:T(8,128)(2,1)S(1)}, u32[]{:S(2)}, u32[]{:S(2)}) collective-permute-start(bf16[3,8,2,32,128]{4,3,2,1,0:T(8,128)(2,1)S(1)} %pad_maximum_fusion.1), channel_id=1, source_target_pairs={{0,2},{32,34},{64,66},{96,98},{2,4},{34,36},{66,68},{98,100},{4,6}... | collective-permute-start | bytes 1179656 | tf_op jit(solution)/shard_map/ppermute | solution.py:251
  62.2 28.3 %collective-permute-start.1 = (bf16[1,8,2,32,128]{4,3,2,1,0:T(8,128)(2,1)S(1)}, bf16[1,8,2,32,128]{4,3,2,1,0:T(8,128)(2,1)S(1)}, u32[]{:S(2)}, u32[]{:S(2)}) collective-permute-start(bf16[1,8,2,32,128]{4,3,2,1,0:T(8,128)(2,1)S(1)} %collective-permute-done.refs_3_), channel_id=1, source_target_pairs={{0,250},{32,154},{64,186},{96,218},{2,252},{34,156},{66,188},{98,2... | collective-permute-start | bytes 393224 | tf_op jit(solution)/shard_map/ppermute | solution.py:251
  90.6 44.6 %collective-permute-start.7 = (bf16[4,8,2,32,128]{4,3,2,1,0:T(8,128)(2,1)S(1)}, bf16[4,8,2,32,128]{4,3,2,1,0:T(8,128)(2,1)S(1)}, u32[]{:S(2)}, u32[]{:S(2)}) collective-permute-start(bf16[4,8,2,32,128]{4,3,2,1,0:T(8,128)(2,1)S(1)} %pad_maximum_fusion), channel_id=1, source_target_pairs={{0,254},{32,158},{64,190},{96,222},{2,0},{34,32},{66,64},{98,96},{... | collective-permute-start | bytes 1572872 | tf_op jit(solution)/shard_map/ppermute | solution.py:251
  92.6 42.6 %collective-permute-start.9 = (bf16[3,8,2,32,128]{4,3,2,1,0:T(8,128)(2,1)S(1)}, bf16[3,8,2,32,128]{4,3,2,1,0:T(8,128)(2,1)S(1)}, u32[]{:S(2)}, u32[]{:S(2)}) collective-permute-start(bf16[3,8,2,32,128]{4,3,2,1,0:T(8,128)(2,1)S(1)} %pad_maximum_fusion.2), channel_id=1, source_target_pairs={{0,2},{32,34},{64,66},{96,98},{2,4},{34,36},{66,68},{98,100},{4,6}... | collective-permute-start | bytes 1179656 | tf_op jit(solution)/shard_map/ppermute | solution.py:251
  97.7 14.8 %copy-start = (s32[16]{0:T(128)S(1)}, s32[16]{0:T(128)}, u32[]{:S(2)}) copy-start(s32[16]{0:T(128)} %refs_0_.7) | copy-start | bytes 196
  97.7 14.8 %all-to-all-start = ((bf16[8,4,32,128]{3,2,1,0:T(8,128)(2,1)}), bf16[8,4,32,128]{3,2,1,0:T(8,128)(2,1)S(1)}, u32[]{:S(2)}, u32[]{:S(2)}) async-start(bf16[8,4,32,128]{3,2,1,0:T(8,128)(2,1)} %shard_map.46), calls=%async_computation | async-start | bytes 524288 | tf_op jit(solution)/shard_map/all_to_all | solution.py:246
  105.3 16.2 %collective-permute-start.2 = (bf16[1,8,2,32,128]{4,3,2,1,0:T(8,128)(2,1)S(1)}, bf16[1,8,2,32,128]{4,3,2,1,0:T(8,128)(2,1)S(1)}, u32[]{:S(2)}, u32[]{:S(2)}) collective-permute-start(bf16[1,8,2,32,128]{4,3,2,1,0:T(8,128)(2,1)S(1)} %collective-permute-done.1.refs_4_), channel_id=1, source_target_pairs={{0,250},{32,154},{64,186},{96,218},{2,252},{34,156},{66,188},{98,2... | collective-permute-start | bytes 393224 | tf_op jit(solution)/shard_map/ppermute | solution.py:251
  121.5 20.6 %collective-permute-start.3 = (bf16[1,8,2,32,128]{4,3,2,1,0:T(8,128)(2,1)S(1)}, bf16[1,8,2,32,128]{4,3,2,1,0:T(8,128)(2,1)S(1)}, u32[]{:S(2)}, u32[]{:S(2)}) collective-permute-start(bf16[1,8,2,32,128]{4,3,2,1,0:T(8,128)(2,1)S(1)} %collective-permute-done.2.refs_4_), channel_id=1, source_target_pairs={{0,254},{32,158},{64,190},{96,222},{2,0},{34,32},{66,64},{98,96},{... | collective-permute-start | bytes 393224 | tf_op jit(solution)/shard_map/ppermute | solution.py:251
  128.9 13.1 %collective-permute-start.4 = (bf16[1,8,2,32,128]{4,3,2,1,0:T(8,128)(2,1)S(1)}, bf16[1,8,2,32,128]{4,3,2,1,0:T(8,128)(2,1)S(1)}, u32[]{:S(2)}, u32[]{:S(2)}) collective-permute-start(bf16[1,8,2,32,128]{4,3,2,1,0:T(8,128)(2,1)S(1)} %collective-permute-done.2.refs_4_), channel_id=1, source_target_pairs={{0,2},{32,34},{64,66},{96,98},{2,4},{34,36},{66,68},{98,100},{4,6}... | collective-permute-start | bytes 393224 | tf_op jit(solution)/shard_map/ppermute | solution.py:251
where the time goes:
time: 158 us
  starting transfers between devices  72.4 us (46%)
  blocking collectives  34.4 us (22%)
  waiting for transfers between devices  29 us (18%)
  Pallas kernels  20.3 us (13%)
    ppermute x10, starting transfers between devices, spread(): back = lax.ppermute(jnp.stack(parts), RING, plan.pairs[name])  64.7 us
    ppermute x10, waiting for transfers between devices, spread(): back = lax.ppermute(jnp.stack(parts), RING, plan.pairs[name])  29 us
    all_to_all x1, blocking collectives, spread(): own = lax.all_to_all(kv, PLANE, split_axis=0, concat_axis=0, tiled=True)  22.6 us
    pallas_call x4, Pallas kernels, attend(): pl.pallas_call(functools.partial(attend_kernel, where, first, last), out_...  17.1 us
    all_to_all x1, blocking collectives, spread(): out = lax.all_to_all(state, PLANE, split_axis=0, concat_axis=0, tiled=True)  11.8 us
    all_to_all x1, starting transfers between devices, spread(): q = lax.all_to_all(q, PLANE, split_axis=0, concat_axis=0, tiled=True)  7.65 us
    pallas_call x2, Pallas kernels, pack(): pl.pallas_call(kernel, out_shape=jax.ShapeDtypeStruct(shape, jnp.bfloat16...  3.25 us
  transfers between devices with their start and end apart: 11, of which 4 were waited for; matrix products, arithmetic and copies ran while one was open for 0% of the time, Pallas kernels for 10%

commit v1 on v0

v1 whole, which is shorter than its diff:
```python
import functools
import math

import jax
import jax.numpy as jnp
from jax import lax
from jax.experimental import pallas as pl
from jax.experimental.pallas import tpu as pltpu
from jax.sharding import Mesh
from jax.sharding import PartitionSpec as P


HD = 128
ROWS = 32
HEADS = 4
CHUNK = 64
NEG_FILL = -1e30
AXES = ("x", "zh", "y", "zl", "c")
PLANE = ("x", "c")
RING = ("zh", "y", "zl")

STEPS = (
    ("m1", (0,), (-9,), -9),
    ("p1", (0,), (3,), 3),
    ("p2", (3,), (6,), 3),
    ("m2", (-9,), (-12,), -3),
    ("e1", (0, 3, 6, -9), (1, 4, 7, -8), 1),
    ("m3", (-12,), (-15,), -3),
    ("g2", (1, 4, -12), (2, 5, -11), 1),
    ("g1", (-9, -12), (-10, -13), -1),
    ("h2", (-15, 7), (-14, 8), 1),
    ("h1", (-15,), (-16,), -1),
)
CALLS = (
    (0, 3, 6),
    (1, 4, 7, -8, -9, -12),
    (2, 5, -10, -11, -13, -15),
    (8, -14, -16),
)


class Plan:
    def __init__(self, outer, half, halves):
        length, chips = half * halves, outer * half
        index = lambda z, y: ((z // half) * outer + y) * half + z % half
        where = {(z, y * half + z % half): index(z, y) for z in range(length) for y in range(outer)}
        held = {0: {key: key for key in where}}
        moves = {}
        for name, sent, got, shift in STEPS:
            target = {}
            for slot, new in zip(sent, got):
                held[new] = {}
                for (z, n), (zs, ns) in held[slot].items():
                    z2 = (z + shift) % length
                    to = (z2, (ns + (z2 - zs) % half) % chips)
                    assert target.setdefault((z, n), to) == to
                    held[new][to] = (zs, ns)
            assert len(set(target.values())) == len(target)
            moves[name] = target
        wanted = {s: {key for key in where if at[key][1] <= key[1]} for s, at in held.items()}
        self.pairs = {}
        for name, sent, got, shift in reversed(STEPS):
            used = {a: b for a, b in moves[name].items() if any(b in wanted[s] for s in got)}
            for slot, new in zip(sent, got):
                wanted[slot] |= {a for a, b in used.items() if b in wanted[new]}
            self.pairs[name] = [(where[a], where[b]) for a, b in sorted(used.items())]
        for (z, n) in where:
            want = {(h * half + m % half, m) for m in range(max(0, n - half // 2), n + 1) for h in range(halves)}
            got = [held[s][z, n] for call in CALLS for s in call]
            assert len(set(got)) == len(got) and want <= set(got)


def row_offsets(shape, dim):
    i = lax.broadcasted_iota(jnp.int32, shape, dim)
    return ((i >> 5) & 1) * 256 + (i >> 6) * 64 + (i & 31)


def document_bounds(lengths):
    count = lengths.shape[0]
    lane = lax.broadcasted_iota(jnp.int32, (1, HD), 1)
    begin = jnp.where(lane == count, -(1 << 24), 1 << 24)
    end = jnp.where(lane == count, 0, -(1 << 24))
    at = jnp.int32(0)
    for d in range(count):
        begin = jnp.where(lane == d, at, begin)
        at = at + lengths[d]
        end = jnp.where(lane == d, at, end)
    return begin, end


def attend_kernel(slots, first, last, *refs):
    count = len(slots)
    refs = list(refs)
    arrays = max(a for _, a, _ in slots) + 1
    if first:
        lengths, q_ref, *refs = refs
    else:
        bounds, q_all, top_in, acc_in, *refs = refs
    kv, refs = refs[:arrays], refs[arrays:]
    if last:
        out_ref, tops, *refs = refs
    elif first:
        bounds, q_all, tops, acc_out, *refs = refs
    else:
        tops, acc_out, *refs = refs
    k_all, v_all, *refs = refs
    scores, rounded = refs[:2], refs[2:]
    unit = math.log2(math.e) / math.sqrt(HD)
    half, halves = lax.axis_size("zl"), lax.axis_size("zh")

    chip = lax.axis_index("y") * half + lax.axis_index("zl")
    zh = lax.axis_index("zh")
    offsets = row_offsets((256, HD), 0)

    def members(base):
        return (offsets >= bounds[0:1] - base) & (offsets < bounds[1:2] - base)

    if first:
        begin, end = document_bounds(lengths)
        bounds[0:1], bounds[1:2] = begin, end
        apart = jnp.where(members(chip * 512 + zh * ROWS), 0.0, NEG_FILL).astype(jnp.bfloat16)
        for h in range(HEADS):
            q_all[h, :, :HD] = q_ref[:, h].reshape(256, HD)
            q_all[h, :, HD:] = apart

    later = {}
    for j, (slot, a, i) in enumerate(slots):
        rows = slice(j * 256, (j + 1) * 256)
        back = slot if slot >= 0 else slot + half
        from_zh = ((zh * half + lax.axis_index("zl") - slot + half * halves) >> 4) & 1
        base = (chip - back) * 512 + from_zh * ROWS
        k_all[rows, :HD] = kv[a][i, :, 0].reshape(256, HD)
        k_all[rows, HD:] = jnp.where(members(base), 1.0, 0.0).astype(jnp.bfloat16)
        v_all[rows, :HD] = kv[a][i, :, 1].reshape(256, HD)
        if back == 0:
            later[j] = (from_zh - zh) * ROWS
    v_all[:, HD:] = jnp.ones((count * 256, HD), jnp.bfloat16)

    def score(h):
        scores[h & 1][...] = lax.dot_general(
            q_all[h], k_all[...], (((1,), (1,)), ((), ())), preferred_element_type=jnp.float32
        )

    def weigh(h):
        for r in range(0, 256, CHUNK):
            rows = slice(r, r + CHUNK)
            wide = None
            for j in range(count):
                cols = slice(j * 256, (j + 1) * 256)
                s = scores[h & 1][rows, cols]
                if j in later:
                    q_at = row_offsets((256, 1), 0)[rows] - later[j]
                    s = jnp.where(row_offsets((1, 256), 1) <= q_at, s, NEG_FILL)
                    scores[h & 1][rows, cols] = s
                wide = s if wide is None else jnp.maximum(wide, s)
            top = jnp.max(wide, axis=1, keepdims=True)
            if not first:
                top = jnp.maximum(top_in[h, rows], top)
            for j in range(count):
                cols = slice(j * 256, (j + 1) * 256)
                w = jnp.exp2((scores[h & 1][rows, cols] - top) * unit)
                rounded[h & 1][rows, cols] = w.astype(jnp.bfloat16)
            tops[h, rows] = top

    def gather(h):
        for r in range(0, 256, 128):
            rows = slice(r, r + 128)
            added = jnp.dot(rounded[h & 1][rows], v_all[...], preferred_element_type=jnp.float32)
            if not first:
                factor = jnp.exp2((top_in[h, rows] - tops[h, rows]) * unit)
                added = added + acc_in[h, rows] * factor
            if last:
                res = added[:, :HD] / added[:, HD:]
                out_ref[r // ROWS : r // ROWS + 4, h] = res.astype(jnp.bfloat16).reshape(4, ROWS, HD)
            else:
                acc_out[h, rows] = added

    for h in range(HEADS + 2):
        if h < HEADS:
            score(h)
        if h >= 2:
            gather(h - 2)
        if 1 <= h <= HEADS:
            weigh(h - 1)


VMEM = pl.BlockSpec(memory_space=pltpu.VMEM)
SMEM = pl.BlockSpec(memory_space=pltpu.SMEM)


def attend(heads_in, slots, blocks, state, last):
    n = len(blocks)
    first = state is None
    bounds = jax.ShapeDtypeStruct((8, HD), jnp.int32)
    q_all = jax.ShapeDtypeStruct((HEADS, 256, 2 * HD), jnp.bfloat16)
    top = jax.ShapeDtypeStruct((HEADS, 256, 1), jnp.float32)
    acc = jax.ShapeDtypeStruct((HEADS, 256, 2 * HD), jnp.float32)
    out = jax.ShapeDtypeStruct((8, HEADS, ROWS, HD), jnp.bfloat16)
    outs = out if last else (bounds, q_all, top, acc) if first else (top, acc)
    arrays = list({id(b): b for b, _ in blocks}.values())
    number = {id(b): a for a, b in enumerate(arrays)}
    where = tuple((s, number[id(b)], i) for s, (b, i) in zip(slots, blocks))
    return pl.pallas_call(
        functools.partial(attend_kernel, where, first, last),
        out_shape=outs,
        in_specs=([SMEM, VMEM] if first else [VMEM] * 4) + [VMEM] * len(arrays),
        out_specs=VMEM if last else tuple(VMEM for _ in outs),
        scratch_shapes=([pltpu.VMEM(top.shape, top.dtype)] if last else [])
        + [
            pltpu.VMEM((n * 256, 2 * HD), jnp.bfloat16),
            pltpu.VMEM((n * 256, 2 * HD), jnp.bfloat16),
            pltpu.VMEM((256, n * 256), jnp.float32),
            pltpu.VMEM((256, n * 256), jnp.float32),
            pltpu.VMEM((256, n * 256), jnp.bfloat16),
            pltpu.VMEM((256, n * 256), jnp.bfloat16),
        ],
        compiler_params=pltpu.CompilerParams(vmem_limit_bytes=(6 + 2 * n) << 20),
        cost_estimate=pl.CostEstimate(
            flops=n * HEADS * 256 * 256 * HD * 4,
            bytes_accessed=n * 131072 + 1500000,
            transcendentals=n * HEADS * 256 * 256,
        ),
    )(*heads_in, *(() if first else state), *arrays)


def pack_kv_kernel(k_ref, v_ref, out_ref):
    for g in range(8):
        out_ref[g, 0] = k_ref[0, :, g * HD : (g + 1) * HD]
        out_ref[g, 1] = v_ref[0, :, g * HD : (g + 1) * HD]


def pack_q_kernel(q_ref, out_ref):
    for g in range(8):
        for h in range(HEADS):
            at = (g * HEADS + h) * HD
            out_ref[g, h] = q_ref[0, :, at : at + HD]


def pack(kernel, shape, *arrays):
    return pl.pallas_call(
        kernel,
        out_shape=jax.ShapeDtypeStruct(shape, jnp.bfloat16),
        in_specs=[VMEM] * len(arrays),
        out_specs=VMEM,
    )(*arrays)


def body(plan, *args):
    return spread(plan, *args)


def spread(plan, queries, keys, values, doc_lengths):
    kv = pack(pack_kv_kernel, (8, 2, ROWS, HD), keys, values)
    own = lax.all_to_all(kv, PLANE, split_axis=0, concat_axis=0, tiled=True)
    q = pack(pack_q_kernel, (8, HEADS, ROWS, HD), queries)
    q = lax.all_to_all(q, PLANE, split_axis=0, concat_axis=0, tiled=True)

    held = {0: (own[None], 0)}
    for name, sent, got, _ in STEPS:
        parts = [held[s][0][held[s][1]] for s in sent]
        back = lax.ppermute(jnp.stack(parts), RING, plan.pairs[name])
        for i, s in enumerate(got):
            held[s] = (back, i)

    heads_in, state = (doc_lengths, q), None
    for j, call in enumerate(CALLS):
        state = attend(heads_in, call, [held[s] for s in call], state, j == len(CALLS) - 1)
        if j == 0:
            heads_in, state = state[:2], state[2:]
    out = lax.all_to_all(state, PLANE, split_axis=0, concat_axis=0, tiled=True)
    return jnp.transpose(out, (2, 0, 1, 3)).reshape(1, ROWS, 32 * HD)


def solution(mesh):
    fine = Mesh(mesh.devices.reshape(4, 2, 4, 16, 2), AXES)
    spec = P(("y", "zl", "c"), ("x", "zh"), None)
    return jax.shard_map(
        functools.partial(body, Plan(4, 16, 2)),
        mesh=fine,
        in_specs=(spec, spec, spec, P()),
        out_specs=spec,
        check_vma=False,
    )
```

time: 158 us -> 125 us (0.79)
  starting transfers between devices: 72.4 us -> 43.7 us
  Pallas kernels: 20.3 us -> 12.3 us
  waiting for transfers between devices: 29 us -> 33.3 us
    ppermute x10, starting transfers between devices: 64.7 us -> 39.2 us  [spread(): back = lax.ppermute(jnp.stack(parts), RING, plan.pairs[name])]
    pallas_call x4, Pallas kernels: 17.1 us -> 9.05 us  [attend(): pl.pallas_call(functools.partial(attend_kernel, where, first, last), out_...]
    ppermute x10, waiting for transfers between devices: 29 us -> 33.3 us  [spread(): back = lax.ppermute(jnp.stack(parts), RING, plan.pairs[name])]
    all_to_all x1, starting transfers between devices: 7.65 us -> 4.53 us  [spread(): q = lax.all_to_all(q, PLANE, split_axis=0, concat_axis=0, tiled=True)]
  transfers between devices with their start and end apart: 11 -> 11, of which waited for: 4 -> 3; matrix products, arithmetic and copies ran while one was open for 0% -> 0% of each run, Pallas kernels for 10% -> 7%
where the time goes in v1:
time: 125 us; the launch traced here: 124 us
  starting transfers between devices  43.7 us (35%)
  blocking collectives  33.6 us (27%)
  waiting for transfers between devices  33.3 us (27%)
  Pallas kernels  12.3 us (10%)
    ppermute x10, starting transfers between devices, spread(): back = lax.ppermute(jnp.stack(parts), RING, plan.pairs[name])  39.2 us
    ppermute x10, waiting for transfers between devices, spread(): back = lax.ppermute(jnp.stack(parts), RING, plan.pairs[name])  33.3 us
    all_to_all x1, blocking collectives, spread(): own = lax.all_to_all(kv, PLANE, split_axis=0, concat_axis=0, tiled=True)  22.6 us
    all_to_all x1, blocking collectives, spread(): out = lax.all_to_all(state, PLANE, split_axis=0, concat_axis=0, tiled=True)  10.9 us
    pallas_call x4, Pallas kernels, attend(): pl.pallas_call(functools.partial(attend_kernel, where, first, last), out_...  9.05 us
    all_to_all x1, starting transfers between devices, spread(): q = lax.all_to_all(q, PLANE, split_axis=0, concat_axis=0, tiled=True)  4.53 us
    pallas_call x2, Pallas kernels, pack(): pl.pallas_call(kernel, out_shape=jax.ShapeDtypeStruct(shape, jnp.bfloat16...  3.25 us
  transfers between devices with their start and end apart: 11, of which 3 were waited for; matrix products, arithmetic and copies ran while one was open for 0% of the time, Pallas kernels for 7%

profile of v1, /device:TPU:1, one launch (start us, length us, event | category | flops | bytes accessed | tf_op | source)
XLA Modules:
  0.0 124.3 jit_solution(6745657680960310405)
XLA Ops:
  0.0 1.5 %shard_map.47 = bf16[8,2,32,128]{3,2,1,0:T(8,128)(2,1)} custom-call(bf16[1,32,1024]{2,1,0:T(8,128)(2,1)} %k_ref.1, bf16[1,32,1024]{2,1,0:T(8,128)(2,1)} %v_ref.1), custom_call_target="tpu_custom_call" | custom-call | tf_op jit(solution)/shard_map/pallas_call | solution.py:240
  1.6 22.6 %all_to_all.15 = bf16[8,2,32,128]{3,2,1,0:T(8,128)(2,1)S(1)} all-to-all(bf16[8,2,32,128]{3,2,1,0:T(8,128)(2,1)} %shard_map.47), channel_id=1, replica_groups=mesh['x'=4,'zh'=2,'y'=4,'zl'=16,'c'=2] {'x','c'}, dimensions={0} | all-to-all | bytes 262144 | tf_op jit(solution)/shard_map/all_to_all | solution.py:254
  24.2 1.3 %collective-permute-start = (bf16[1,8,2,32,128]{4,3,2,1,0:T(8,128)(2,1)S(1)}, bf16[1,8,2,32,128]{4,3,2,1,0:T(8,128)(2,1)S(1)}, u32[]{:S(2)}, u32[]{:S(2)}) collective-permute-start(bf16[1,8,2,32,128]{4,3,2,1,0:T(8,128)(2,1)S(1)} %bitcast.2), channel_id=1, source_target_pairs={{0,6},{32,38},{64,70},{96,102},{2,8},{34,40},{66,72},{98,104},{4,1... | collective-permute-start | bytes 393224 | tf_op jit(solution)/shard_map/ppermute | solution.py:261
  25.5 15.0 %collective-permute-start.2 = (bf16[1,8,2,32,128]{4,3,2,1,0:T(8,128)(2,1)S(1)}, bf16[1,8,2,32,128]{4,3,2,1,0:T(8,128)(2,1)S(1)}, u32[]{:S(2)}, u32[]{:S(2)}) collective-permute-start(bf16[1,8,2,32,128]{4,3,2,1,0:T(8,128)(2,1)S(1)} %bitcast.3), channel_id=1, source_target_pairs={{0,142},{32,174},{64,206},{96,238},{2,144},{34,176},{66,208},{98,2... | collective-permute-start | bytes 393224 | tf_op jit(solution)/shard_map/ppermute | solution.py:261
  40.5 0.0 collective-permute-done.refs_3_
  40.5 0.7 collective-permute-start.1
  41.2 25.9 %collective-permute-done.2.refs_5_ = bf16[1,8,2,32,128]{4,3,2,1,0:T(8,128)(2,1)S(1)} collective-permute-done((bf16[1,8,2,32,128]{4,3,2,1,0:T(8,128)(2,1)S(1)}, bf16[1,8,2,32,128]{4,3,2,1,0:T(8,128)(2,1)S(1)}, u32[]{:S(2)}, u32[]{:S(2)}) %collective-permute-start.2) | collective-permute-done | bytes 131104 | tf_op jit(solution)/shard_map/ppermute | solution.py:261
  67.1 0.0 collective-permute-done.1.refs_4_
  67.1 0.1 pad_maximum_fusion
  67.2 1.3 %collective-permute-start.3 = (bf16[4,8,2,32,128]{4,3,2,1,0:T(8,128)(2,1)S(1)}, bf16[4,8,2,32,128]{4,3,2,1,0:T(8,128)(2,1)S(1)}, u32[]{:S(2)}, u32[]{:S(2)}) collective-permute-start(bf16[4,8,2,32,128]{4,3,2,1,0:T(8,128)(2,1)S(1)} %pad_maximum_fusion), channel_id=1, source_target_pairs={{0,2},{32,34},{64,66},{96,98},{2,4},{34,36},{66,68},{98,100},{4,6}... | collective-permute-start | bytes 1572872 | tf_op jit(solution)/shard_map/ppermute | solution.py:261
  68.5 5.3 %collective-permute-start.4 = (bf16[1,8,2,32,128]{4,3,2,1,0:T(8,128)(2,1)S(1)}, bf16[1,8,2,32,128]{4,3,2,1,0:T(8,128)(2,1)S(1)}, u32[]{:S(2)}, u32[]{:S(2)}) collective-permute-start(bf16[1,8,2,32,128]{4,3,2,1,0:T(8,128)(2,1)S(1)} %collective-permute-done.2.refs_5_), channel_id=1, source_target_pairs={{0,250},{32,154},{64,186},{96,218},{2,252},{34,156},{66,188},{98,2... | collective-permute-start | bytes 393224 | tf_op jit(solution)/shard_map/ppermute | solution.py:261
  73.8 1.7 %shard_map.46 = bf16[8,4,32,128]{3,2,1,0:T(8,128)(2,1)} custom-call(bf16[1,32,4096]{2,1,0:T(8,128)(2,1)} %q_ref.1), custom_call_target="tpu_custom_call" | custom-call | tf_op jit(solution)/shard_map/pallas_call | solution.py:240
  75.5 4.5 %all-to-all-start = ((bf16[8,4,32,128]{3,2,1,0:T(8,128)(2,1)}), bf16[8,4,32,128]{3,2,1,0:T(8,128)(2,1)S(1)}, u32[]{:S(2)}, u32[]{:S(2)}) async-start(bf16[8,4,32,128]{3,2,1,0:T(8,128)(2,1)} %shard_map.46), calls=%async_computation | async-start | bytes 524288 | tf_op jit(solution)/shard_map/all_to_all | solution.py:256
  80.0 2.7 %collective-permute-done.4.refs_6_ = bf16[1,8,2,32,128]{4,3,2,1,0:T(8,128)(2,1)S(1)} collective-permute-done((bf16[1,8,2,32,128]{4,3,2,1,0:T(8,128)(2,1)S(1)}, bf16[1,8,2,32,128]{4,3,2,1,0:T(8,128)(2,1)S(1)}, u32[]{:S(2)}, u32[]{:S(2)}) %collective-permute-start.4) | collective-permute-done | bytes 131104 | tf_op jit(solution)/shard_map/ppermute | solution.py:261
  82.7 10.5 %collective-permute-start.7 = (bf16[1,8,2,32,128]{4,3,2,1,0:T(8,128)(2,1)S(1)}, bf16[1,8,2,32,128]{4,3,2,1,0:T(8,128)(2,1)S(1)}, u32[]{:S(2)}, u32[]{:S(2)}) collective-permute-start(bf16[1,8,2,32,128]{4,3,2,1,0:T(8,128)(2,1)S(1)} %collective-permute-done.4.refs_6_), channel_id=1, source_target_pairs={{0,250},{32,154},{64,186},{96,218},{2,252},{34,156},{66,188},{98,2... | collective-permute-start | bytes 393224 | tf_op jit(solution)/shard_map/ppermute | solution.py:261
  93.2 0.0 collective-permute-done.3.refs_4_
  93.2 0.7 collective-permute-start.5
  94.0 1.3 %collective-permute-start.6 = (bf16[2,8,2,32,128]{4,3,2,1,0:T(8,128)(2,1)S(1)}, bf16[2,8,2,32,128]{4,3,2,1,0:T(8,128)(2,1)S(1)}, u32[]{:S(2)}, u32[]{:S(2)}) collective-permute-start(bf16[2,8,2,32,128]{4,3,2,1,0:T(8,128)(2,1)S(1)} %pad_maximum_fusion.2), channel_id=1, source_target_pairs={{0,254},{32,158},{64,190},{96,222},{34,32},{66,64},{98,96},{36,34}... | collective-permute-start | bytes 786440 | tf_op jit(solution)/shard_map/ppermute | solution.py:261
  95.3 0.0 copy-start
  95.3 4.7 %collective-permute-done.7.refs_6_ = bf16[1,8,2,32,128]{4,3,2,1,0:T(8,128)(2,1)S(1)} collective-permute-done((bf16[1,8,2,32,128]{4,3,2,1,0:T(8,128)(2,1)S(1)}, bf16[1,8,2,32,128]{4,3,2,1,0:T(8,128)(2,1)S(1)}, u32[]{:S(2)}, u32[]{:S(2)}) %collective-permute-start.7) | collective-permute-done | bytes 131104 | tf_op jit(solution)/shard_map/ppermute | solution.py:261
  100.0 0.7 collective-permute-start.8
  100.7 0.0 all-to-all-done.refs_1_
  100.7 0.0 copy-done
  100.7 2.0 %shard_map.48 = (s32[8,128]{1,0:T(8,128)S(1)}, bf16[4,256,256]{2,1,0:T(8,128)(2,1)S(1)}, f32[4,256,1]{2,1,0:T(8,128)S(1)}, f32[4,256,256]{2,1,0:T(8,128)S(1)}) custom-call(s32[16]{0:T(128)S(1)} %copy-done, bf16[8,4,32,128]{3,2,1,0:T(8,128)(2,1)S(1)} %all-to-all-done.refs_1_, bf16[1,8,2,32,128]{4,3,2,1,0:T(8,128)(2,1)S(1)} %bitcast.5, ...), custom_call_target="tpu_custom_call" | custom-call | flops 402653184 | bytes 1893216 | tf_op jit(solution)/shard_map/pallas_call | solution.py:203
  102.7 2.5 %collective-permute-start.9 = (bf16[1,8,2,32,128]{4,3,2,1,0:T(8,128)(2,1)S(1)}, bf16[1,8,2,32,128]{4,3,2,1,0:T(8,128)(2,1)S(1)}, u32[]{:S(2)}, u32[]{:S(2)}) collective-permute-start(bf16[1,8,2,32,128]{4,3,2,1,0:T(8,128)(2,1)S(1)} %collective-permute-done.7.refs_6_), channel_id=1, source_target_pairs={{0,254},{32,158},{64,190},{96,222},{2,0},{34,32},{66,64},{98,96},{... | collective-permute-start | bytes 393224 | tf_op jit(solution)/shard_map/ppermute | solution.py:261
  105.2 2.6 %shard_map.49 = (f32[4,256,1]{2,1,0:T(8,128)S(1)}, f32[4,256,256]{2,1,0:T(8,128)S(1)}) custom-call(s32[8,128]{1,0:T(8,128)S(1)} %get-tuple-element.13.refs_0_, bf16[4,256,256]{2,1,0:T(8,128)(2,1)S(1)} %get-tuple-element.14.refs_1_, f32[4,256,1]{2,1,0:T(8,128)S(1)} %get-tuple-element.15.refs_2_, f32[4,256,256]{2,1,0:T(8,128)S(1)} %get-tuple-element.16.refs_3_, ...), custom_call_target="tpu_custom_call" | custom-call | flops 805306368 | bytes 2286432 | tf_op jit(solution)/shard_map/pallas_call | solution.py:203
  107.8 0.0 collective-permute-done.6.refs_5_
  107.8 0.0 collective-permute-done.5.refs_4_
  107.8 2.6 %shard_map.50 = (f32[4,256,1]{2,1,0:T(8,128)S(1)}, f32[4,256,256]{2,1,0:T(8,128)S(1)}) custom-call(s32[8,128]{1,0:T(8,128)S(1)} %get-tuple-element.13.refs_0_, bf16[4,256,256]{2,1,0:T(8,128)(2,1)S(1)} %get-tuple-element.14.refs_1_, f32[4,256,1]{2,1,0:T(8,128)S(1)} %get-tuple-element.17.refs_2_, f32[4,256,256]{2,1,0:T(8,128)S(1)} %get-tuple-element.18.refs_3_, ...), custom_call_target="tpu_custom_call" | custom-call | flops 805306368 | bytes 2286432 | tf_op jit(solution)/shard_map/pallas_call | solution.py:203
  110.4 0.0 collective-permute-done.9.refs_5_
  110.5 0.0 collective-permute-done.8.refs_4_
  110.5 1.9 %shard_map.51 = bf16[8,4,32,128]{3,2,1,0:T(8,128)(2,1)S(1)} custom-call(s32[8,128]{1,0:T(8,128)S(1)} %get-tuple-element.13.refs_0_, bf16[4,256,256]{2,1,0:T(8,128)(2,1)S(1)} %get-tuple-element.14.refs_1_, f32[4,256,1]{2,1,0:T(8,128)S(1)} %get-tuple-element.19.refs_2_, f32[4,256,256]{2,1,0:T(8,128)S(1)} %get-tuple-element.20.refs_3_, ...), custom_call_target="tpu_custom_call" | custom-call | flops 402653184 | bytes 1893216 | tf_op jit(solution)/shard_map/pallas_call | solution.py:203
  112.3 10.9 %all_to_all.16 = bf16[8,4,32,128]{3,2,1,0:T(8,128)(2,1)S(1)} all-to-all(bf16[8,4,32,128]{3,2,1,0:T(8,128)(2,1)S(1)} %shard_map.51), channel_id=1, replica_groups=mesh['x'=4,'zh'=2,'y'=4,'zl'=16,'c'=2] {'x','c'}, dimensions={0} | all-to-all | bytes 524288 | tf_op jit(solution)/shard_map/all_to_all | solution.py:270
  123.3 0.1 copy.5
  123.4 0.9 reshape.3
  (5 shorter events, 0.1 us)
Async XLA Ops:
  24.2 16.3 %collective-permute-start = (bf16[1,8,2,32,128]{4,3,2,1,0:T(8,128)(2,1)S(1)}, bf16[1,8,2,32,128]{4,3,2,1,0:T(8,128)(2,1)S(1)}, u32[]{:S(2)}, u32[]{:S(2)}) collective-permute-start(bf16[1,8,2,32,128]{4,3,2,1,0:T(8,128)(2,1)S(1)} %bitcast.2), channel_id=1, source_target_pairs={{0,6},{32,38},{64,70},{96,102},{2,8},{34,40},{66,72},{98,104},{4,1... | collective-permute-start | bytes 393224 | tf_op jit(solution)/shard_map/ppermute | solution.py:261
  25.5 41.6 %collective-permute-start.2 = (bf16[1,8,2,32,128]{4,3,2,1,0:T(8,128)(2,1)S(1)}, bf16[1,8,2,32,128]{4,3,2,1,0:T(8,128)(2,1)S(1)}, u32[]{:S(2)}, u32[]{:S(2)}) collective-permute-start(bf16[1,8,2,32,128]{4,3,2,1,0:T(8,128)(2,1)S(1)} %bitcast.3), channel_id=1, source_target_pairs={{0,142},{32,174},{64,206},{96,238},{2,144},{34,176},{66,208},{98,2... | collective-permute-start | bytes 393224 | tf_op jit(solution)/shard_map/ppermute | solution.py:261
  40.5 26.6 %collective-permute-start.1 = (bf16[1,8,2,32,128]{4,3,2,1,0:T(8,128)(2,1)S(1)}, bf16[1,8,2,32,128]{4,3,2,1,0:T(8,128)(2,1)S(1)}, u32[]{:S(2)}, u32[]{:S(2)}) collective-permute-start(bf16[1,8,2,32,128]{4,3,2,1,0:T(8,128)(2,1)S(1)} %collective-permute-done.refs_3_), channel_id=1, source_target_pairs={{32,38},{64,70},{96,102},{34,40},{66,72},{98,104},{36,42},{68,74},... | collective-permute-start | bytes 393224 | tf_op jit(solution)/shard_map/ppermute | solution.py:261
  67.2 26.0 %collective-permute-start.3 = (bf16[4,8,2,32,128]{4,3,2,1,0:T(8,128)(2,1)S(1)}, bf16[4,8,2,32,128]{4,3,2,1,0:T(8,128)(2,1)S(1)}, u32[]{:S(2)}, u32[]{:S(2)}) collective-permute-start(bf16[4,8,2,32,128]{4,3,2,1,0:T(8,128)(2,1)S(1)} %pad_maximum_fusion), channel_id=1, source_target_pairs={{0,2},{32,34},{64,66},{96,98},{2,4},{34,36},{66,68},{98,100},{4,6}... | collective-permute-start | bytes 1572872 | tf_op jit(solution)/shard_map/ppermute | solution.py:261
  68.5 14.2 %collective-permute-start.4 = (bf16[1,8,2,32,128]{4,3,2,1,0:T(8,128)(2,1)S(1)}, bf16[1,8,2,32,128]{4,3,2,1,0:T(8,128)(2,1)S(1)}, u32[]{:S(2)}, u32[]{:S(2)}) collective-permute-start(bf16[1,8,2,32,128]{4,3,2,1,0:T(8,128)(2,1)S(1)} %collective-permute-done.2.refs_5_), channel_id=1, source_target_pairs={{0,250},{32,154},{64,186},{96,218},{2,252},{34,156},{66,188},{98,2... | collective-permute-start | bytes 393224 | tf_op jit(solution)/shard_map/ppermute | solution.py:261
  75.5 25.3 %all-to-all-start = ((bf16[8,4,32,128]{3,2,1,0:T(8,128)(2,1)}), bf16[8,4,32,128]{3,2,1,0:T(8,128)(2,1)S(1)}, u32[]{:S(2)}, u32[]{:S(2)}) async-start(bf16[8,4,32,128]{3,2,1,0:T(8,128)(2,1)} %shard_map.46), calls=%async_computation | async-start | bytes 524288 | tf_op jit(solution)/shard_map/all_to_all | solution.py:256
  82.7 17.4 %collective-permute-start.7 = (bf16[1,8,2,32,128]{4,3,2,1,0:T(8,128)(2,1)S(1)}, bf16[1,8,2,32,128]{4,3,2,1,0:T(8,128)(2,1)S(1)}, u32[]{:S(2)}, u32[]{:S(2)}) collective-permute-start(bf16[1,8,2,32,128]{4,3,2,1,0:T(8,128)(2,1)S(1)} %collective-permute-done.4.refs_6_), channel_id=1, source_target_pairs={{0,250},{32,154},{64,186},{96,218},{2,252},{34,156},{66,188},{98,2... | collective-permute-start | bytes 393224 | tf_op jit(solution)/shard_map/ppermute | solution.py:261
  93.2 14.6 %collective-permute-start.5 = (bf16[3,8,2,32,128]{4,3,2,1,0:T(8,128)(2,1)S(1)}, bf16[3,8,2,32,128]{4,3,2,1,0:T(8,128)(2,1)S(1)}, u32[]{:S(2)}, u32[]{:S(2)}) collective-permute-start(bf16[3,8,2,32,128]{4,3,2,1,0:T(8,128)(2,1)S(1)} %pad_maximum_fusion.1), channel_id=1, source_target_pairs={{32,34},{64,66},{96,98},{2,4},{34,36},{66,68},{98,100},{4,6},{36,3... | collective-permute-start | bytes 1179656 | tf_op jit(solution)/shard_map/ppermute | solution.py:261
  94.0 13.8 %collective-permute-start.6 = (bf16[2,8,2,32,128]{4,3,2,1,0:T(8,128)(2,1)S(1)}, bf16[2,8,2,32,128]{4,3,2,1,0:T(8,128)(2,1)S(1)}, u32[]{:S(2)}, u32[]{:S(2)}) collective-permute-start(bf16[2,8,2,32,128]{4,3,2,1,0:T(8,128)(2,1)S(1)} %pad_maximum_fusion.2), channel_id=1, source_target_pairs={{0,254},{32,158},{64,190},{96,222},{34,32},{66,64},{98,96},{36,34}... | collective-permute-start | bytes 786440 | tf_op jit(solution)/shard_map/ppermute | solution.py:261
  95.3 5.4 %copy-start = (s32[16]{0:T(128)S(1)}, s32[16]{0:T(128)}, u32[]{:S(2)}) copy-start(s32[16]{0:T(128)} %refs_0_.1) | copy-start | bytes 196
  100.0 10.4 %collective-permute-start.8 = (bf16[2,8,2,32,128]{4,3,2,1,0:T(8,128)(2,1)S(1)}, bf16[2,8,2,32,128]{4,3,2,1,0:T(8,128)(2,1)S(1)}, u32[]{:S(2)}, u32[]{:S(2)}) collective-permute-start(bf16[2,8,2,32,128]{4,3,2,1,0:T(8,128)(2,1)S(1)} %pad_maximum_fusion.3), channel_id=1, source_target_pairs={{32,34},{64,66},{96,98},{2,4},{34,36},{66,68},{98,100},{4,6},{36,3... | collective-permute-start | bytes 786440 | tf_op jit(solution)/shard_map/ppermute | solution.py:261
  102.7 7.7 %collective-permute-start.9 = (bf16[1,8,2,32,128]{4,3,2,1,0:T(8,128)(2,1)S(1)}, bf16[1,8,2,32,128]{4,3,2,1,0:T(8,128)(2,1)S(1)}, u32[]{:S(2)}, u32[]{:S(2)}) collective-permute-start(bf16[1,8,2,32,128]{4,3,2,1,0:T(8,128)(2,1)S(1)} %collective-permute-done.7.refs_6_), channel_id=1, source_target_pairs={{0,254},{32,158},{64,190},{96,222},{2,0},{34,32},{66,64},{98,96},{... | collective-permute-start | bytes 393224 | tf_op jit(solution)/shard_map/ppermute | solution.py:261

commit v2 on v1

--- a/solution.py
+++ b/solution.py
@@ -23,19 +23,20 @@
     ("m1", (0,), (-9,), -9),
     ("p1", (0,), (3,), 3),
     ("p2", (3,), (6,), 3),
+    ("e1", (0, 3), (1, 4), 1),
     ("m2", (-9,), (-12,), -3),
-    ("e1", (0, 3, 6, -9), (1, 4, 7, -8), 1),
+    ("e2", (6, -9), (7, -8), 1),
     ("m3", (-12,), (-15,), -3),
-    ("g2", (1, 4, -12), (2, 5, -11), 1),
+    ("g2", (1, 4, 7, -12), (2, 5, 8, -11), 1),
     ("g1", (-9, -12), (-10, -13), -1),
-    ("h2", (-15, 7), (-14, 8), 1),
+    ("h2", (-15,), (-14,), 1),
     ("h1", (-15,), (-16,), -1),
 )
 CALLS = (
     (0, 3, 6),
     (1, 4, 7, -8, -9, -12),
-    (2, 5, -10, -11, -13, -15),
-    (8, -14, -16),
+    (2, 5, 8, -10, -11, -13, -15),
+    (-14, -16),
 )
 
 
@@ -258,6 +259,8 @@
     held = {0: (own[None], 0)}
     for name, sent, got, _ in STEPS:
         parts = [held[s][0][held[s][1]] for s in sent]
+        if len(parts) > 1:
+            parts = lax.optimization_barrier(parts)
         back = lax.ppermute(jnp.stack(parts), RING, plan.pairs[name])
         for i, s in enumerate(got):
             held[s] = (back, i)

time: 125 us -> 139 us (1.11)
  the two profiles are of different devices: /device:TPU:1 before, /device:TPU:16 now
where the time goes in v2:
time: 139 us; the launch traced here: 138 us
  starting transfers between devices  60.8 us (44%)
  waiting for transfers between devices  41.7 us (30%)
  blocking collectives  22.2 us (16%)
  Pallas kernels  12 us (9%)
    ppermute x11, starting transfers between devices, spread(): back = lax.ppermute(jnp.stack(parts), RING, plan.pairs[name])  57.4 us
    ppermute x11, waiting for transfers between devices, spread(): back = lax.ppermute(jnp.stack(parts), RING, plan.pairs[name])  41.7 us
    all_to_all x1, blocking collectives, spread(): out = lax.all_to_all(state, PLANE, split_axis=0, concat_axis=0, tiled=True)  11.8 us
    all_to_all x1, blocking collectives, spread(): own = lax.all_to_all(kv, PLANE, split_axis=0, concat_axis=0, tiled=True)  10.4 us
    pallas_call x4, Pallas kernels, attend(): pl.pallas_call(functools.partial(attend_kernel, where, first, last), out_...  8.75 us
    all_to_all x1, starting transfers between devices, spread(): q = lax.all_to_all(q, PLANE, split_axis=0, concat_axis=0, tiled=True)  3.41 us
    pallas_call x2, Pallas kernels, pack(): pl.pallas_call(kernel, out_shape=jax.ShapeDtypeStruct(shape, jnp.bfloat16...  3.25 us
  transfers between devices with their start and end apart: 12, of which 4 were waited for; matrix products, arithmetic and copies ran while one was open for 0% of the time, Pallas kernels for 7%

profile of v2, /device:TPU:16, one launch (start us, length us, event | category | flops | bytes accessed | tf_op | source)
XLA Modules:
  0.0 138.2 jit_solution(9856174725812753705)
XLA Ops:
  0.0 1.5 %shard_map.47 = bf16[8,2,32,128]{3,2,1,0:T(8,128)(2,1)} custom-call(bf16[1,32,1024]{2,1,0:T(8,128)(2,1)} %k_ref.1, bf16[1,32,1024]{2,1,0:T(8,128)(2,1)} %v_ref.1), custom_call_target="tpu_custom_call" | custom-call | tf_op jit(solution)/shard_map/pallas_call | solution.py:241
  1.6 10.4 %all_to_all.15 = bf16[8,2,32,128]{3,2,1,0:T(8,128)(2,1)S(1)} all-to-all(bf16[8,2,32,128]{3,2,1,0:T(8,128)(2,1)} %shard_map.47), channel_id=1, replica_groups=mesh['x'=4,'zh'=2,'y'=4,'zl'=16,'c'=2] {'x','c'}, dimensions={0} | all-to-all | bytes 262144 | tf_op jit(solution)/shard_map/all_to_all | solution.py:255
  11.9 6.5 %collective-permute-start = (bf16[1,8,2,32,128]{4,3,2,1,0:T(8,128)(2,1)S(1)}, bf16[1,8,2,32,128]{4,3,2,1,0:T(8,128)(2,1)S(1)}, u32[]{:S(2)}, u32[]{:S(2)}) collective-permute-start(bf16[1,8,2,32,128]{4,3,2,1,0:T(8,128)(2,1)S(1)} %bitcast.22), channel_id=1, source_target_pairs={{0,6},{32,38},{64,70},{96,102},{2,8},{34,40},{66,72},{98,104},{4,1... | collective-permute-start | bytes 393224 | tf_op jit(solution)/shard_map/ppermute | solution.py:264
  18.5 22.0 %collective-permute-start.3 = (bf16[1,8,2,32,128]{4,3,2,1,0:T(8,128)(2,1)S(1)}, bf16[1,8,2,32,128]{4,3,2,1,0:T(8,128)(2,1)S(1)}, u32[]{:S(2)}, u32[]{:S(2)}) collective-permute-start(bf16[1,8,2,32,128]{4,3,2,1,0:T(8,128)(2,1)S(1)} %bitcast.23), channel_id=1, source_target_pairs={{0,142},{32,174},{64,206},{96,238},{2,144},{34,176},{66,208},{98,2... | collective-permute-start | bytes 393224 | tf_op jit(solution)/shard_map/ppermute | solution.py:264
  40.4 0.0 collective-permute-done.refs_3_
  40.5 2.6 %collective-permute-start.1 = (bf16[1,8,2,32,128]{4,3,2,1,0:T(8,128)(2,1)S(1)}, bf16[1,8,2,32,128]{4,3,2,1,0:T(8,128)(2,1)S(1)}, u32[]{:S(2)}, u32[]{:S(2)}) collective-permute-start(bf16[1,8,2,32,128]{4,3,2,1,0:T(8,128)(2,1)S(1)} %collective-permute-done.refs_3_), channel_id=1, source_target_pairs={{32,38},{64,70},{96,102},{34,40},{66,72},{98,104},{36,42},{68,74},... | collective-permute-start | bytes 393224 | tf_op jit(solution)/shard_map/ppermute | solution.py:264
  43.1 4.1 %collective-permute-start.2 = (bf16[2,8,2,32,128]{4,3,2,1,0:T(8,128)(2,1)S(1)}, bf16[2,8,2,32,128]{4,3,2,1,0:T(8,128)(2,1)S(1)}, u32[]{:S(2)}, u32[]{:S(2)}) collective-permute-start(bf16[2,8,2,32,128]{4,3,2,1,0:T(8,128)(2,1)S(1)} %pad_maximum_fusion.1), channel_id=1, source_target_pairs={{0,2},{32,34},{64,66},{96,98},{2,4},{34,36},{66,68},{98,100},{4,6}... | collective-permute-start | bytes 786440 | tf_op jit(solution)/shard_map/ppermute | solution.py:264
  47.3 17.3 %collective-permute-done.3.refs_6_ = bf16[1,8,2,32,128]{4,3,2,1,0:T(8,128)(2,1)S(1)} collective-permute-done((bf16[1,8,2,32,128]{4,3,2,1,0:T(8,128)(2,1)S(1)}, bf16[1,8,2,32,128]{4,3,2,1,0:T(8,128)(2,1)S(1)}, u32[]{:S(2)}, u32[]{:S(2)}) %collective-permute-start.3) | collective-permute-done | bytes 131104 | tf_op jit(solution)/shard_map/ppermute | solution.py:264
  64.6 0.0 collective-permute-done.1.refs_4_
  64.6 1.9 %collective-permute-start.4 = (bf16[2,8,2,32,128]{4,3,2,1,0:T(8,128)(2,1)S(1)}, bf16[2,8,2,32,128]{4,3,2,1,0:T(8,128)(2,1)S(1)}, u32[]{:S(2)}, u32[]{:S(2)}) collective-permute-start(bf16[2,8,2,32,128]{4,3,2,1,0:T(8,128)(2,1)S(1)} %pad_maximum_fusion.2), channel_id=1, source_target_pairs={{32,34},{64,66},{96,98},{34,36},{66,68},{98,100},{36,38},{68,70},{... | collective-permute-start | bytes 786440 | tf_op jit(solution)/shard_map/ppermute | solution.py:264
  66.5 1.9 %collective-permute-start.5 = (bf16[1,8,2,32,128]{4,3,2,1,0:T(8,128)(2,1)S(1)}, bf16[1,8,2,32,128]{4,3,2,1,0:T(8,128)(2,1)S(1)}, u32[]{:S(2)}, u32[]{:S(2)}) collective-permute-start(bf16[1,8,2,32,128]{4,3,2,1,0:T(8,128)(2,1)S(1)} %collective-permute-done.3.refs_6_), channel_id=1, source_target_pairs={{0,250},{32,154},{64,186},{96,218},{2,252},{34,156},{66,188},{98,2... | collective-permute-start | bytes 393224 | tf_op jit(solution)/shard_map/ppermute | solution.py:264
  68.4 0.0 collective-permute-done.2.refs_4_
  68.5 8.2 %collective-permute-done.4.refs_5_ = bf16[2,8,2,32,128]{4,3,2,1,0:T(8,128)(2,1)S(1)} collective-permute-done((bf16[2,8,2,32,128]{4,3,2,1,0:T(8,128)(2,1)S(1)}, bf16[2,8,2,32,128]{4,3,2,1,0:T(8,128)(2,1)S(1)}, u32[]{:S(2)}, u32[]{:S(2)}) %collective-permute-start.4) | collective-permute-done | bytes 262176 | tf_op jit(solution)/shard_map/ppermute | solution.py:264
  76.7 4.5 %collective-permute-done.5.refs_7_ = bf16[1,8,2,32,128]{4,3,2,1,0:T(8,128)(2,1)S(1)} collective-permute-done((bf16[1,8,2,32,128]{4,3,2,1,0:T(8,128)(2,1)S(1)}, bf16[1,8,2,32,128]{4,3,2,1,0:T(8,128)(2,1)S(1)}, u32[]{:S(2)}, u32[]{:S(2)}) %collective-permute-start.5) | collective-permute-done | bytes 131104 | tf_op jit(solution)/shard_map/ppermute | solution.py:264
  81.2 0.1 pad_maximum_fusion
  81.3 2.5 %collective-permute-start.6 = (bf16[4,8,2,32,128]{4,3,2,1,0:T(8,128)(2,1)S(1)}, bf16[4,8,2,32,128]{4,3,2,1,0:T(8,128)(2,1)S(1)}, u32[]{:S(2)}, u32[]{:S(2)}) collective-permute-start(bf16[4,8,2,32,128]{4,3,2,1,0:T(8,128)(2,1)S(1)} %pad_maximum_fusion), channel_id=1, source_target_pairs={{32,34},{64,66},{96,98},{2,4},{34,36},{66,68},{98,100},{4,6},{36,3... | collective-permute-start | bytes 1572872 | tf_op jit(solution)/shard_map/ppermute | solution.py:264
  83.8 1.7 %shard_map.46 = bf16[8,4,32,128]{3,2,1,0:T(8,128)(2,1)} custom-call(bf16[1,32,4096]{2,1,0:T(8,128)(2,1)} %q_ref.1), custom_call_target="tpu_custom_call" | custom-call | tf_op jit(solution)/shard_map/pallas_call | solution.py:241
  85.5 3.4 %all-to-all-start = ((bf16[8,4,32,128]{3,2,1,0:T(8,128)(2,1)}), bf16[8,4,32,128]{3,2,1,0:T(8,128)(2,1)S(1)}, u32[]{:S(2)}, u32[]{:S(2)}) async-start(bf16[8,4,32,128]{3,2,1,0:T(8,128)(2,1)} %shard_map.46), calls=%async_computation | async-start | bytes 524288 | tf_op jit(solution)/shard_map/all_to_all | solution.py:257
  88.9 0.0 copy-start
  88.9 5.5 %collective-permute-start.7 = (bf16[2,8,2,32,128]{4,3,2,1,0:T(8,128)(2,1)S(1)}, bf16[2,8,2,32,128]{4,3,2,1,0:T(8,128)(2,1)S(1)}, u32[]{:S(2)}, u32[]{:S(2)}) collective-permute-start(bf16[2,8,2,32,128]{4,3,2,1,0:T(8,128)(2,1)S(1)} %pad_maximum_fusion.3), channel_id=1, source_target_pairs={{0,254},{32,158},{64,190},{96,222},{34,32},{66,64},{98,96},{36,34}... | collective-permute-start | bytes 786440 | tf_op jit(solution)/shard_map/ppermute | solution.py:264
  94.4 2.4 %collective-permute-start.8 = (bf16[1,8,2,32,128]{4,3,2,1,0:T(8,128)(2,1)S(1)}, bf16[1,8,2,32,128]{4,3,2,1,0:T(8,128)(2,1)S(1)}, u32[]{:S(2)}, u32[]{:S(2)}) collective-permute-start(bf16[1,8,2,32,128]{4,3,2,1,0:T(8,128)(2,1)S(1)} %collective-permute-done.5.refs_7_), channel_id=1, source_target_pairs={{0,250},{32,154},{64,186},{96,218},{2,252},{34,156},{66,188},{98,2... | collective-permute-start | bytes 393224 | tf_op jit(solution)/shard_map/ppermute | solution.py:264
  96.9 0.0 all-to-all-done.refs_1_
  96.9 0.0 copy-done
  96.9 2.0 %shard_map.48 = (s32[8,128]{1,0:T(8,128)S(1)}, bf16[4,256,256]{2,1,0:T(8,128)(2,1)S(1)}, f32[4,256,1]{2,1,0:T(8,128)S(1)}, f32[4,256,256]{2,1,0:T(8,128)S(1)}) custom-call(s32[16]{0:T(128)S(1)} %copy-done, bf16[8,4,32,128]{3,2,1,0:T(8,128)(2,1)S(1)} %all-to-all-done.refs_1_, bf16[1,8,2,32,128]{4,3,2,1,0:T(8,128)(2,1)S(1)} %bitcast.25, ...), custom_call_target="tpu_custom_call" | custom-call | flops 402653184 | bytes 1893216 | tf_op jit(solution)/shard_map/pallas_call | solution.py:204
  98.9 11.7 %collective-permute-done.8.refs_6_ = bf16[1,8,2,32,128]{4,3,2,1,0:T(8,128)(2,1)S(1)} collective-permute-done((bf16[1,8,2,32,128]{4,3,2,1,0:T(8,128)(2,1)S(1)}, bf16[1,8,2,32,128]{4,3,2,1,0:T(8,128)(2,1)S(1)}, u32[]{:S(2)}, u32[]{:S(2)}) %collective-permute-start.8) | collective-permute-done | bytes 131104 | tf_op jit(solution)/shard_map/ppermute | solution.py:264
  110.5 1.9 %collective-permute-start.9 = (bf16[1,8,2,32,128]{4,3,2,1,0:T(8,128)(2,1)S(1)}, bf16[1,8,2,32,128]{4,3,2,1,0:T(8,128)(2,1)S(1)}, u32[]{:S(2)}, u32[]{:S(2)}) collective-permute-start(bf16[1,8,2,32,128]{4,3,2,1,0:T(8,128)(2,1)S(1)} %collective-permute-done.8.refs_6_), channel_id=1, source_target_pairs={{32,34},{64,66},{96,98},{2,4},{34,36},{66,68},{98,100},{4,6},{36,3... | collective-permute-start | bytes 393224 | tf_op jit(solution)/shard_map/ppermute | solution.py:264
  112.5 6.0 %collective-permute-start.10 = (bf16[1,8,2,32,128]{4,3,2,1,0:T(8,128)(2,1)S(1)}, bf16[1,8,2,32,128]{4,3,2,1,0:T(8,128)(2,1)S(1)}, u32[]{:S(2)}, u32[]{:S(2)}) collective-permute-start(bf16[1,8,2,32,128]{4,3,2,1,0:T(8,128)(2,1)S(1)} %collective-permute-done.8.refs_6_), channel_id=1, source_target_pairs={{0,254},{32,158},{64,190},{96,222},{2,0},{34,32},{66,64},{98,96},{... | collective-permute-start | bytes 393224 | tf_op jit(solution)/shard_map/ppermute | solution.py:264
  118.5 2.5 %shard_map.49 = (f32[4,256,1]{2,1,0:T(8,128)S(1)}, f32[4,256,256]{2,1,0:T(8,128)S(1)}) custom-call(s32[8,128]{1,0:T(8,128)S(1)} %get-tuple-element.23.refs_0_, bf16[4,256,256]{2,1,0:T(8,128)(2,1)S(1)} %get-tuple-element.24.refs_1_, f32[4,256,1]{2,1,0:T(8,128)S(1)} %get-tuple-element.25.refs_2_, f32[4,256,256]{2,1,0:T(8,128)S(1)} %get-tuple-element.26.refs_3_, ...), custom_call_target="tpu_custom_call" | custom-call | flops 805306368 | bytes 2286432 | tf_op jit(solution)/shard_map/pallas_call | solution.py:204
  121.0 0.0 collective-permute-done.7.refs_5_
  121.0 0.0 collective-permute-done.6.refs_4_
  121.1 2.9 %shard_map.50 = (f32[4,256,1]{2,1,0:T(8,128)S(1)}, f32[4,256,256]{2,1,0:T(8,128)S(1)}) custom-call(s32[8,128]{1,0:T(8,128)S(1)} %get-tuple-element.23.refs_0_, bf16[4,256,256]{2,1,0:T(8,128)(2,1)S(1)} %get-tuple-element.24.refs_1_, f32[4,256,1]{2,1,0:T(8,128)S(1)} %get-tuple-element.31.refs_2_, f32[4,256,256]{2,1,0:T(8,128)S(1)} %get-tuple-element.32.refs_3_, ...), custom_call_target="tpu_custom_call" | custom-call | flops 939524096 | bytes 2417504 | tf_op jit(solution)/shard_map/pallas_call | solution.py:204
  123.9 0.0 collective-permute-done.9.refs_4_
  123.9 0.0 collective-permute-done.10.refs_5_
  124.0 1.4 shard_map.51
  125.3 11.8 %all_to_all.16 = bf16[8,4,32,128]{3,2,1,0:T(8,128)(2,1)S(1)} all-to-all(bf16[8,4,32,128]{3,2,1,0:T(8,128)(2,1)S(1)} %shard_map.51), channel_id=1, replica_groups=mesh['x'=4,'zh'=2,'y'=4,'zl'=16,'c'=2] {'x','c'}, dimensions={0} | all-to-all | bytes 524288 | tf_op jit(solution)/shard_map/all_to_all | solution.py:273
  137.1 0.1 copy.5
  137.3 0.9 reshape.3
  (5 shorter events, 0.1 us)
Async XLA Ops:
  11.9 28.5 %collective-permute-start = (bf16[1,8,2,32,128]{4,3,2,1,0:T(8,128)(2,1)S(1)}, bf16[1,8,2,32,128]{4,3,2,1,0:T(8,128)(2,1)S(1)}, u32[]{:S(2)}, u32[]{:S(2)}) collective-permute-start(bf16[1,8,2,32,128]{4,3,2,1,0:T(8,128)(2,1)S(1)} %bitcast.22), channel_id=1, source_target_pairs={{0,6},{32,38},{64,70},{96,102},{2,8},{34,40},{66,72},{98,104},{4,1... | collective-permute-start | bytes 393224 | tf_op jit(solution)/shard_map/ppermute | solution.py:264
  18.5 46.1 %collective-permute-start.3 = (bf16[1,8,2,32,128]{4,3,2,1,0:T(8,128)(2,1)S(1)}, bf16[1,8,2,32,128]{4,3,2,1,0:T(8,128)(2,1)S(1)}, u32[]{:S(2)}, u32[]{:S(2)}) collective-permute-start(bf16[1,8,2,32,128]{4,3,2,1,0:T(8,128)(2,1)S(1)} %bitcast.23), channel_id=1, source_target_pairs={{0,142},{32,174},{64,206},{96,238},{2,144},{34,176},{66,208},{98,2... | collective-permute-start | bytes 393224 | tf_op jit(solution)/shard_map/ppermute | solution.py:264
  40.5 24.1 %collective-permute-start.1 = (bf16[1,8,2,32,128]{4,3,2,1,0:T(8,128)(2,1)S(1)}, bf16[1,8,2,32,128]{4,3,2,1,0:T(8,128)(2,1)S(1)}, u32[]{:S(2)}, u32[]{:S(2)}) collective-permute-start(bf16[1,8,2,32,128]{4,3,2,1,0:T(8,128)(2,1)S(1)} %collective-permute-done.refs_3_), channel_id=1, source_target_pairs={{32,38},{64,70},{96,102},{34,40},{66,72},{98,104},{36,42},{68,74},... | collective-permute-start | bytes 393224 | tf_op jit(solution)/shard_map/ppermute | solution.py:264
  43.1 25.3 %collective-permute-start.2 = (bf16[2,8,2,32,128]{4,3,2,1,0:T(8,128)(2,1)S(1)}, bf16[2,8,2,32,128]{4,3,2,1,0:T(8,128)(2,1)S(1)}, u32[]{:S(2)}, u32[]{:S(2)}) collective-permute-start(bf16[2,8,2,32,128]{4,3,2,1,0:T(8,128)(2,1)S(1)} %pad_maximum_fusion.1), channel_id=1, source_target_pairs={{0,2},{32,34},{64,66},{96,98},{2,4},{34,36},{66,68},{98,100},{4,6}... | collective-permute-start | bytes 786440 | tf_op jit(solution)/shard_map/ppermute | solution.py:264
  64.6 12.1 %collective-permute-start.4 = (bf16[2,8,2,32,128]{4,3,2,1,0:T(8,128)(2,1)S(1)}, bf16[2,8,2,32,128]{4,3,2,1,0:T(8,128)(2,1)S(1)}, u32[]{:S(2)}, u32[]{:S(2)}) collective-permute-start(bf16[2,8,2,32,128]{4,3,2,1,0:T(8,128)(2,1)S(1)} %pad_maximum_fusion.2), channel_id=1, source_target_pairs={{32,34},{64,66},{96,98},{34,36},{66,68},{98,100},{36,38},{68,70},{... | collective-permute-start | bytes 786440 | tf_op jit(solution)/shard_map/ppermute | solution.py:264
  66.5 14.7 %collective-permute-start.5 = (bf16[1,8,2,32,128]{4,3,2,1,0:T(8,128)(2,1)S(1)}, bf16[1,8,2,32,128]{4,3,2,1,0:T(8,128)(2,1)S(1)}, u32[]{:S(2)}, u32[]{:S(2)}) collective-permute-start(bf16[1,8,2,32,128]{4,3,2,1,0:T(8,128)(2,1)S(1)} %collective-permute-done.3.refs_6_), channel_id=1, source_target_pairs={{0,250},{32,154},{64,186},{96,218},{2,252},{34,156},{66,188},{98,2... | collective-permute-start | bytes 393224 | tf_op jit(solution)/shard_map/ppermute | solution.py:264
  81.3 39.8 %collective-permute-start.6 = (bf16[4,8,2,32,128]{4,3,2,1,0:T(8,128)(2,1)S(1)}, bf16[4,8,2,32,128]{4,3,2,1,0:T(8,128)(2,1)S(1)}, u32[]{:S(2)}, u32[]{:S(2)}) collective-permute-start(bf16[4,8,2,32,128]{4,3,2,1,0:T(8,128)(2,1)S(1)} %pad_maximum_fusion), channel_id=1, source_target_pairs={{32,34},{64,66},{96,98},{2,4},{34,36},{66,68},{98,100},{4,6},{36,3... | collective-permute-start | bytes 1572872 | tf_op jit(solution)/shard_map/ppermute | solution.py:264
  85.5 11.4 %all-to-all-start = ((bf16[8,4,32,128]{3,2,1,0:T(8,128)(2,1)}), bf16[8,4,32,128]{3,2,1,0:T(8,128)(2,1)S(1)}, u32[]{:S(2)}, u32[]{:S(2)}) async-start(bf16[8,4,32,128]{3,2,1,0:T(8,128)(2,1)} %shard_map.46), calls=%async_computation | async-start | bytes 524288 | tf_op jit(solution)/shard_map/all_to_all | solution.py:257
  88.9 8.0 %copy-start = (s32[16]{0:T(128)S(1)}, s32[16]{0:T(128)}, u32[]{:S(2)}) copy-start(s32[16]{0:T(128)} %refs_0_.1) | copy-start | bytes 196
  88.9 32.1 %collective-permute-start.7 = (bf16[2,8,2,32,128]{4,3,2,1,0:T(8,128)(2,1)S(1)}, bf16[2,8,2,32,128]{4,3,2,1,0:T(8,128)(2,1)S(1)}, u32[]{:S(2)}, u32[]{:S(2)}) collective-permute-start(bf16[2,8,2,32,128]{4,3,2,1,0:T(8,128)(2,1)S(1)} %pad_maximum_fusion.3), channel_id=1, source_target_pairs={{0,254},{32,158},{64,190},{96,222},{34,32},{66,64},{98,96},{36,34}... | collective-permute-start | bytes 786440 | tf_op jit(solution)/shard_map/ppermute | solution.py:264
  94.4 16.1 %collective-permute-start.8 = (bf16[1,8,2,32,128]{4,3,2,1,0:T(8,128)(2,1)S(1)}, bf16[1,8,2,32,128]{4,3,2,1,0:T(8,128)(2,1)S(1)}, u32[]{:S(2)}, u32[]{:S(2)}) collective-permute-start(bf16[1,8,2,32,128]{4,3,2,1,0:T(8,128)(2,1)S(1)} %collective-permute-done.5.refs_7_), channel_id=1, source_target_pairs={{0,250},{32,154},{64,186},{96,218},{2,252},{34,156},{66,188},{98,2... | collective-permute-start | bytes 393224 | tf_op jit(solution)/shard_map/ppermute | solution.py:264
  110.5 13.4 %collective-permute-start.9 = (bf16[1,8,2,32,128]{4,3,2,1,0:T(8,128)(2,1)S(1)}, bf16[1,8,2,32,128]{4,3,2,1,0:T(8,128)(2,1)S(1)}, u32[]{:S(2)}, u32[]{:S(2)}) collective-permute-start(bf16[1,8,2,32,128]{4,3,2,1,0:T(8,128)(2,1)S(1)} %collective-permute-done.8.refs_6_), channel_id=1, source_target_pairs={{32,34},{64,66},{96,98},{2,4},{34,36},{66,68},{98,100},{4,6},{36,3... | collective-permute-start | bytes 393224 | tf_op jit(solution)/shard_map/ppermute | solution.py:264
  112.5 11.5 %collective-permute-start.10 = (bf16[1,8,2,32,128]{4,3,2,1,0:T(8,128)(2,1)S(1)}, bf16[1,8,2,32,128]{4,3,2,1,0:T(8,128)(2,1)S(1)}, u32[]{:S(2)}, u32[]{:S(2)}) collective-permute-start(bf16[1,8,2,32,128]{4,3,2,1,0:T(8,128)(2,1)S(1)} %collective-permute-done.8.refs_6_), channel_id=1, source_target_pairs={{0,254},{32,158},{64,190},{96,222},{2,0},{34,32},{66,64},{98,96},{... | collective-permute-start | bytes 393224 | tf_op jit(solution)/shard_map/ppermute | solution.py:264
